TPU v7x, 8 devices: a whole 2x2x1 slice. The times are simulated.
8 devices in a mesh: mp: 2 (over z, y), dp: 4 (over x, core).
Axes of the slice: x: 2, y: 2, z: 1, core: 2. Of those that a mesh axis runs over, the one named last changes fastest.
Arguments:
- a_mat: bfloat16 [4096, 65536], P(('mp', 'dp'))
- b_mat: bfloat16 [65536, 4096], P(('mp', 'dp'))
Outputs:
- output: bfloat16 [4096, 4096], P(('mp', 'dp'))
All inputs are finite; a program needn't handle non-finite values.
Results may differ from a plain program's by a relative error of at most 0.001.
Values are sent between devices in bfloat16 or wider.
A program may use at most 1 GiB of HBM per device.

v0:
```python
import jax
import jax.numpy as jnp
from jax import lax
from jax.sharding import PartitionSpec as P


def solution(mesh):
    mp_size = mesh.shape["mp"]
    dp_size = mesh.shape["dp"]

    def local_product(a_rows, b_rows):
        row_count = a_rows.shape[0]
        tok_piece = b_rows.shape[0]
        a_split = a_rows.reshape(row_count, mp_size, dp_size, tok_piece)
        a_cols = lax.all_to_all(a_split, "dp", 2, 0, tiled=True)
        a_cols = a_cols.reshape(row_count * dp_size, mp_size, tok_piece)
        b_group = lax.all_gather(b_rows, "mp", axis=0, tiled=False)
        part_sum = jnp.einsum("rit,itn->rn", a_cols, b_group, preferred_element_type=jnp.float32)
        row_sum = lax.psum_scatter(part_sum, "dp", scatter_dimension=0, tiled=True)
        return row_sum.astype(jnp.bfloat16)

    return jax.shard_map(
        local_product,
        mesh=mesh,
        in_specs=(P(("mp", "dp"), None), P(("mp", "dp"), None)),
        out_specs=P(("mp", "dp"), None),
        check_vma=False,
    )
```

profile of v0, /device:TPU:0, one launch (start us, length us, event | category | flops | bytes accessed | tf_op | source)
XLA Modules:
  0.0 2067.0 jit_solution(16676499487353892048)
XLA Ops:
  6.5 0.0 all-gather.3.cloned.1.call-start
  6.5 0.7 all-gather.3.cloned.1.call-update
  7.3 0.0 reduce-scatter.2.cloned.1.call-start
  7.3 86.6 %copy.5 = bf16[512,65536]{0,1:T(8,128)(2,1)} copy(bf16[512,65536]{1,0:T(8,128)(2,1)} %param.2) | data formatting | bytes 134217728 | tf_op args[0]
  93.9 79.1 %copy.6 = bf16[512,2,4,8192]{3,0,1,2:T(8,128)(2,1)} copy(bf16[512,2,4,8192]{0,3,2,1:T(8,128)(2,1)} %bitcast) | data formatting | bytes 134217728 | tf_op jit(solution)/shard_map/reshape | solution.py:14
  173.0 755.5 %all_to_all.15 = bf16[512,2,4,8192]{3,0,1,2:T(8,128)(2,1)} all-to-all(bf16[512,2,4,8192]{3,0,1,2:T(8,128)(2,1)} %copy.6), channel_id=1, replica_groups=mesh['mp'=2,'dp'=4] {'dp'}, dimensions={2} | all-to-all | bytes 134217728 | tf_op jit(solution)/shard_map/all_to_all | solution.py:15
  928.5 44.6 %copy.7 = bf16[4,512,2,1,8192]{4,1,0,2,3:T(8,128)(2,1)} copy(bf16[4,512,2,1,8192]{4,1,2,0,3:T(8,128)(2,1)} %bitcast.2) | data formatting | bytes 134217728 | tf_op jit(solution)/shard_map/all_to_all | solution.py:15
  973.1 557.1 %all-gather.3.cloned.1.call-done = bf16[16384,4096]{1,0:T(8,128)(2,1)} async-done(((bf16[8192,4096]{1,0:T(8,128)(2,1)}), bf16[16384,4096]{1,0:T(8,128)(2,1)}) %all-gather.3.cloned.1.call-update) | async-done | bytes 134217744 | tf_op jit(solution)/shard_map/all_gather | solution.py:17
  1530.1 297.9 %convolution_bitcast_fusion = f32[2048,4096]{1,0:T(8,128)} fusion(bf16[2048,2,8192]{2,0,1:T(8,128)(2,1)} %bitcast.3, bf16[2,8192,4096]{2,1,0:T(8,128)(2,1)} %bitcast.4), kind=kOutput, calls=%fused_computation | convolution fusion | flops 274877906944 | bytes 234881024 | tf_op jit(solution)/shard_map/rit,itn->rn/dot_general | solution.py:18
  1828.0 0.0 reduce-scatter.2.cloned.1.call-update
  1828.0 226.2 %reduce-scatter.2.cloned.1.call-done = f32[512,4096]{1,0:T(8,128)} async-done(((f32[2048,4096]{1,0:T(8,128)}), f32[512,4096]{1,0:T(8,128)}) %reduce-scatter.2.cloned.1.call-update) | async-done | bytes 8388624 | tf_op jit(solution)/shard_map/reduce_scatter | solution.py:19
  2054.2 6.0 convert_element_type.3
Async XLA Ops:
  6.5 1523.6 %all-gather.3.cloned.1.call-start = ((), (), s32[]{:S(2)}) async-start(), calls=%async_computation.3 | async-start | bytes 201326592 | tf_op jit(solution)/shard_map/all_gather | solution.py:17
  7.3 2046.9 %reduce-scatter.2.cloned.1.call-start = ((), (), s32[]{:S(2)}) async-start(), calls=%async_computation.2 | async-start | bytes 41943040 | tf_op jit(solution)/shard_map/reduce_scatter | solution.py:19
Sparse Core Ops, SparseCore 0:
  8.8 1521.2 all-gather.2
  1828.1 225.9 reduce-scatter.1
where the time goes:
time: 2070 us
  waiting for transfers between devices  784 us (38%)
  blocking collectives  755 us (36%)
  matrix products  298 us (14%)
  local copies, waits for them, and re-layouts  210 us (10%)
    all_to_all x1, blocking collectives, local_product(): a_cols = lax.all_to_all(a_split, 'dp', 2, 0, tiled=True)  755 us
    all_gather x1, waiting for transfers between devices, local_product(): b_group = lax.all_gather(b_rows, 'mp', axis=0, tiled=False)  557 us
    dot_general x1, matrix products, local_product(): jnp.einsum('rit,itn->rn', a_cols, b_group, preferred_element_type=jnp.flo...  298 us
    reduce_scatter x1, waiting for transfers between devices, local_product(): row_sum = lax.psum_scatter(part_sum, 'dp', scatter_dimension=0, tiled=True)  226 us
    unnamed x1, local copies, waits for them, and re-layouts  86.6 us
    reshape x1, local copies, waits for them, and re-layouts, local_product(): a_split = a_rows.reshape(row_count, mp_size, dp_size, tok_piece)  79.1 us
    all_to_all x1, local copies, waits for them, and re-layouts, local_product(): a_cols = lax.all_to_all(a_split, 'dp', 2, 0, tiled=True)  44.6 us
  transfers between devices with their start and end apart: 2, of which 2 were waited for; matrix products, arithmetic and copies ran while one was open for 10% of the time, Pallas kernels for 0%

commit v1 on v0

v1 whole, which is shorter than its diff:
```python
import functools

import jax
import jax.numpy as jnp
from jax import lax
from jax.experimental import pallas as pl
from jax.experimental.pallas import tpu as pltpu
from jax.sharding import PartitionSpec as P

MESH = pl.DeviceIdType.MESH
N_TILES = 8
K_TILES = 4
WINDOW = 2
MIX_LAG = 2
END_LAG = 4
BUFS = END_LAG + 1
B_PIECES = 8


def _kernel(chunk, a_ref, b_ref, c_ref, b_par, a_in, leg1, leg2,
            a_v, b_v, acc, t1, t2, t3, c_v,
            bx_send, bx_recv, a_send, a_recv, l1_send, l1_recv, l2_send, l2_recv,
            a_sem, b_sem, t_sem, c_sem):
    rows = a_ref.shape[0]
    half_k, cols = b_ref.shape
    chip_k = 2 * half_k
    steps = rows // chunk
    nt = cols // N_TILES
    kt = chip_k // K_TILES
    own_tiles = K_TILES // 2

    mp = lax.axis_index("mp")
    dp = lax.axis_index("dp")
    core = lax.rem(dp, 2)
    xx = dp // 2
    flip_x = (1 - xx) * 2 + core
    flip_y = 1 - mp

    def coords(slot):
        is_x = 1 - slot // 2
        is_y = (slot + 1) // 2
        return mp + is_y * (1 - 2 * mp), xx + is_x * (1 - 2 * xx)

    barrier = pltpu.get_barrier_semaphore()
    for peer in ((mp, flip_x), (flip_y, dp), (flip_y, flip_x), (mp, xx * 2 + 1 - core)):
        pl.semaphore_signal(barrier, inc=1, device_id=peer, device_id_type=MESH)
    pl.semaphore_wait(barrier, 4)

    piece = half_k // B_PIECES

    def b_copy(j):
        span = pl.ds(j * piece, piece)
        return pltpu.make_async_remote_copy(
            src_ref=b_ref.at[span], dst_ref=b_par.at[span],
            send_sem=bx_send.at[j], recv_sem=bx_recv.at[j],
            device_id=(mp, xx * 2 + 1 - core), device_id_type=MESH)

    def a_copy(t, order):
        if order == 2:
            slot = 2
        else:
            slot = core if order == 0 else 1 - core
        to_mp, to_x = coords(slot)
        start = pl.multiple_of((to_mp * 2 + to_x) * chip_k, chip_k)
        span = pl.ds(pl.multiple_of(t * chunk, chunk), chunk)
        return pltpu.make_async_remote_copy(
            src_ref=a_ref.at[span, pl.ds(start, chip_k)],
            dst_ref=a_in.at[slot, span],
            send_sem=a_send.at[t, slot], recv_sem=a_recv.at[t, slot],
            device_id=(to_mp, to_x * 2 + core), device_id_type=MESH)

    def b_tile(n, k):
        src = b_ref if k < own_tiles else b_par
        return pltpu.make_async_copy(
            src.at[pl.ds((k % own_tiles) * kt, kt), pl.ds(pl.multiple_of(n * nt, nt), nt)],
            b_v.at[k], b_sem.at[k])

    for t in range(WINDOW):
        for order in range(3):
            a_copy(t, order).start()
    for j in range(B_PIECES):
        b_copy(j).start()
    for k in range(own_tiles):
        b_tile(0, k).start()
    for j in range(B_PIECES):
        b_copy(j).wait_recv()
    for k in range(own_tiles, K_TILES):
        b_tile(0, k).start()

    def leg1_copy(t):
        odd = lax.rem(t, 2)
        to_mp = mp + odd * (1 - 2 * mp)
        to_x = xx + (1 - odd) * (1 - 2 * xx)
        return pltpu.make_async_remote_copy(
            src_ref=acc.at[lax.rem(t, BUFS), pl.ds(pl.multiple_of((1 + odd) * chunk, chunk), 2 * chunk)],
            dst_ref=leg1.at[t], send_sem=l1_send.at[t], recv_sem=l1_recv.at[t],
            device_id=(to_mp, to_x * 2 + core), device_id_type=MESH)

    def leg2_copy(t):
        odd = lax.rem(t, 2)
        to_mp = mp + (1 - odd) * (1 - 2 * mp)
        to_x = xx + odd * (1 - 2 * xx)
        group = 3 - 2 * odd
        return pltpu.make_async_remote_copy(
            src_ref=acc.at[lax.rem(t, BUFS), pl.ds(pl.multiple_of(group * chunk, chunk), chunk)],
            dst_ref=leg2.at[t], send_sem=l2_send.at[t], recv_sem=l2_recv.at[t],
            device_id=(to_mp, to_x * 2 + core), device_id_type=MESH)

    def c_copy(t):
        slot = lax.rem(t, 2)
        return pltpu.make_async_copy(
            c_v.at[slot], c_ref.at[pl.ds(pl.multiple_of(t * chunk, chunk), chunk)], c_sem.at[slot])

    my_start = (mp * 2 + xx) * chip_k

    def product(t):
        for order in range(3):
            a_copy(t, order).wait_recv()

        span = pl.ds(pl.multiple_of(t * chunk, chunk), chunk)
        loads = []
        for h in range(2):
            off = (core + h - 2 * core * h) * half_k
            for g in range(4):
                if g == 0:
                    src = a_ref.at[span, pl.ds(pl.multiple_of(my_start + off, half_k), half_k)]
                else:
                    src = a_in.at[g - 1, span, pl.ds(pl.multiple_of(off, half_k), half_k)]
                loads.append(pltpu.make_async_copy(
                    src, a_v.at[pl.ds(g * chunk, chunk), pl.ds(h * half_k, half_k)],
                    a_sem.at[h * 4 + g]))
        for load in loads:
            load.start()

        for order in range(3):
            a_copy(t, order).wait_send()

        @pl.when(t + WINDOW < steps)
        def _():
            for order in range(3):
                a_copy(t + WINDOW, order).start()

        for load in loads:
            load.wait()

        buf = lax.rem(t, BUFS)

        def column(n, carry):
            place = pl.ds(pl.multiple_of(n * nt, nt), nt)
            for k in range(K_TILES):
                b_tile(n, k).wait()
                term = jnp.dot(a_v[:, k * kt:(k + 1) * kt], b_v[k],
                               preferred_element_type=jnp.float32)
                if k == 0:
                    acc[buf, :, place] = term
                else:
                    acc[buf, :, place] += term

                @pl.when(t * N_TILES + n < steps * N_TILES - 1)
                def _():
                    b_tile(lax.rem(n + 1, N_TILES), k).start()
            return carry

        lax.fori_loop(0, N_TILES, column, 0)
        leg1_copy(t).start()

    def forward(t):
        odd = lax.rem(t, 2)
        leg1_copy(t).wait_recv()
        load = pltpu.make_async_copy(
            leg1.at[t, pl.ds(pl.multiple_of((1 - odd) * chunk, chunk), chunk)], t1, t_sem.at[0])
        load.start()
        load.wait()
        group = 3 - 2 * odd
        place = pl.ds(pl.multiple_of(group * chunk, chunk), chunk)
        buf = lax.rem(t, BUFS)
        acc[buf, place] += t1[...]
        leg2_copy(t).start()

    def finish(t):
        odd = lax.rem(t, 2)
        leg2_copy(t).wait_recv()
        one = pltpu.make_async_copy(
            leg1.at[t, pl.ds(pl.multiple_of(odd * chunk, chunk), chunk)], t2, t_sem.at[1])
        two = pltpu.make_async_copy(leg2.at[t], t3, t_sem.at[2])
        one.start()
        two.start()

        @pl.when(t >= 2)
        def _():
            c_copy(t).wait()

        one.wait()
        two.wait()
        total = acc[lax.rem(t, BUFS), pl.ds(0, chunk)] + t2[...] + t3[...]
        c_v[lax.rem(t, 2)] = total.astype(c_v.dtype)
        leg1_copy(t).wait_send()
        leg2_copy(t).wait_send()
        c_copy(t).start()

    def step(s, carry):
        @pl.when(s < steps)
        def _():
            product(s)

        @pl.when((s >= MIX_LAG) & (s < steps + MIX_LAG))
        def _():
            forward(s - MIX_LAG)

        @pl.when(s >= END_LAG)
        def _():
            finish(s - END_LAG)
        return carry

    lax.fori_loop(0, steps + END_LAG, step, 0)
    for t in (steps - 2, steps - 1):
        c_copy(t).wait()
    for j in range(B_PIECES):
        b_copy(j).wait_send()


def _product(a_rows, b_rows, chunk):
    rows = a_rows.shape[0]
    half_k, cols = b_rows.shape
    steps = rows // chunk
    nt, kt = cols // N_TILES, 2 * half_k // K_TILES
    sem = pltpu.SemaphoreType.DMA
    hbm = pl.BlockSpec(memory_space=pl.ANY)
    outs = pl.pallas_call(
        functools.partial(_kernel, chunk),
        out_shape=(
            jax.ShapeDtypeStruct((rows, cols), jnp.bfloat16),
            jax.ShapeDtypeStruct((half_k, cols), jnp.bfloat16),
            jax.ShapeDtypeStruct((3, rows, 2 * half_k), jnp.bfloat16),
            jax.ShapeDtypeStruct((steps, 2 * chunk, cols), jnp.float32),
            jax.ShapeDtypeStruct((steps, chunk, cols), jnp.float32),
        ),
        in_specs=[hbm] * 2,
        out_specs=(hbm,) * 5,
        scratch_shapes=[
            pltpu.VMEM((4 * chunk, 2 * half_k), jnp.bfloat16),
            pltpu.VMEM((K_TILES, kt, nt), jnp.bfloat16),
            pltpu.VMEM((BUFS, 4 * chunk, cols), jnp.float32),
            pltpu.VMEM((chunk, cols), jnp.float32),
            pltpu.VMEM((chunk, cols), jnp.float32),
            pltpu.VMEM((chunk, cols), jnp.float32),
            pltpu.VMEM((2, chunk, cols), jnp.bfloat16),
            sem((B_PIECES,)), sem((B_PIECES,)),
            sem((steps, 3)), sem((steps, 3)),
            sem((steps,)), sem((steps,)), sem((steps,)), sem((steps,)),
            sem((8,)), sem((K_TILES,)), sem((3,)), sem((2,)),
        ],
        compiler_params=pltpu.CompilerParams(
            collective_id=0, has_side_effects=True, vmem_limit_bytes=60 << 20),
    )(a_rows, b_rows)
    return outs[0]


def solution(mesh):
    spec = P(("mp", "dp"), None)

    def local(a_rows, b_rows):
        return _product(a_rows, b_rows, min(32, a_rows.shape[0] // 4))

    return jax.shard_map(local, mesh=mesh, in_specs=(spec, spec), out_specs=spec, check_vma=False)
```

time: 2070 us -> 1030 us (0.50)
  Pallas kernels: 0 us -> 1030 us
  waiting for transfers between devices: 784 us -> 0 us
  blocking collectives: 755 us -> 0 us
  matrix products: 298 us -> 0 us
  local copies, waits for them, and re-layouts: 210 us -> 4.7 us
    pallas_call x0 -> x1, Pallas kernels: none -> 1030 us  [_product(): pl.pallas_call(functools.partial(_kernel, chunk), out_shape=(jax.ShapeDty...]
    all_to_all x1 -> x0, blocking collectives: 755 us -> none  [local_product(): a_cols = lax.all_to_all(a_split, 'dp', 2, 0, tiled=True)]
    all_gather x1 -> x0, waiting for transfers between devices: 557 us -> none  [local_product(): b_group = lax.all_gather(b_rows, 'mp', axis=0, tiled=False)]
    dot_general x1 -> x0, matrix products: 298 us -> none  [local_product(): jnp.einsum('rit,itn->rn', a_cols, b_group, preferred_element_type=jnp.flo...]
    reduce_scatter x1 -> x0, waiting for transfers between devices: 226 us -> none  [local_product(): row_sum = lax.psum_scatter(part_sum, 'dp', scatter_dimension=0, tiled=True)]
    unnamed x1, local copies, waits for them, and re-layouts: 86.6 us -> 4.7 us
    reshape x1 -> x0, local copies, waits for them, and re-layouts: 79.1 us -> none  [local_product(): a_split = a_rows.reshape(row_count, mp_size, dp_size, tok_piece)]
    all_to_all x1 -> x0, local copies, waits for them, and re-layouts: 44.6 us -> none  [local_product(): a_cols = lax.all_to_all(a_split, 'dp', 2, 0, tiled=True)]
  transfers between devices with their start and end apart: 2 -> 0, of which waited for: 2 -> 0; matrix products, arithmetic and copies ran while one was open for 10% -> 0% of each run, Pallas kernels for 0% -> 0%
where the time goes in v1:
time: 1030 us
  Pallas kernels  1030 us (100%)
    pallas_call x1, Pallas kernels, _product(): pl.pallas_call(functools.partial(_kernel, chunk), out_shape=(jax.ShapeDty...  1030 us

profile of v1, /device:TPU:0, one launch (start us, length us, event | category | flops | bytes accessed | tf_op | source)
XLA Modules:
  0.0 1030.4 jit_solution(9104152352612741293)
XLA Ops:
  0.0 1025.7 %shard_map.28 = (bf16[512,4096]{1,0:T(8,128)(2,1)}, bf16[8192,4096]{1,0:T(8,128)(2,1)}, bf16[3,512,16384]{2,1,0:T(8,128)(2,1)}, f32[16,64,4096]{2,1,0:T(8,128)}, f32[16,32,4096]{2,1,0:T(8,128)}) custom-call(bf16[512,65536]{1,0:T(8,128)(2,1)} %a_ref.1, bf16[8192,4096]{1,0:T(8,128)(2,1)} %b_ref.1), custom_call_target="tpu_custom_call" | custom-call | tf_op jit(solution)/shard_map/pallas_call | solution.py:229
  1025.7 4.7 copy.4

commit v2 on v0

v2 whole, which is shorter than its diff:
```python
import functools

import jax
import jax.numpy as jnp
from jax import lax
from jax.experimental import pallas as pl
from jax.experimental.pallas import tpu as pltpu
from jax.sharding import PartitionSpec as P

MESH = pl.DeviceIdType.MESH
N_TILES = 8
SLICES = 4
SLOTS = 4
AHEAD = 2
BUFS = 3
B_PIECES = 8


def _kernel(chunk, a_ref, b_ref, c_ref, b_par, a_in, leg1, leg2,
            a_v, b_v, acc, t1, t2, t3, c_v,
            bx_send, bx_recv, a_send, a_recv, l1_send, l1_recv, l2_send, l2_recv,
            a_sem, b_sem, t_sem, c_sem):
    rows = a_ref.shape[0]
    half_k, cols = b_ref.shape
    chip_k = 2 * half_k
    steps = rows // chunk
    half = chunk // 2
    nt = cols // N_TILES
    kt = chip_k // SLICES
    own_slices = SLICES // 2

    mp = lax.axis_index("mp")
    dp = lax.axis_index("dp")
    core = lax.rem(dp, 2)
    xx = dp // 2
    x_peer = (mp, (1 - xx) * 2 + core)
    y_peer = (1 - mp, dp)
    diagonal = (1 - mp, (1 - xx) * 2 + core)
    partner = (mp, xx * 2 + 1 - core)

    barrier = pltpu.get_barrier_semaphore()
    for peer in (x_peer, y_peer, diagonal, partner):
        pl.semaphore_signal(barrier, inc=1, device_id=peer, device_id_type=MESH)
    pl.semaphore_wait(barrier, 4)

    def chunk_rows(t):
        return pl.ds(pl.multiple_of(t * chunk, chunk), chunk)

    def slice_start(q):
        h = q // own_slices
        side = core + h - 2 * core * h
        return side * half_k + lax.rem(q, own_slices) * kt

    piece = half_k // B_PIECES

    def b_copy(j):
        span = pl.ds(j * piece, piece)
        return pltpu.make_async_remote_copy(
            src_ref=b_ref.at[span], dst_ref=b_par.at[span],
            send_sem=bx_send.at[j], recv_sem=bx_recv.at[j],
            device_id=partner, device_id_type=MESH)

    def a_copy(t, q, order):
        slot = 2 if order == 2 else (core if order == 0 else 1 - core)
        is_x = 1 - slot // 2
        is_y = (slot + 1) // 2
        to_mp = mp + is_y * (1 - 2 * mp)
        to_x = xx + is_x * (1 - 2 * xx)
        part = slice_start(q)
        start = pl.multiple_of((to_mp * 2 + to_x) * chip_k + part, kt)
        return pltpu.make_async_remote_copy(
            src_ref=a_ref.at[chunk_rows(t), pl.ds(start, kt)],
            dst_ref=a_in.at[slot, chunk_rows(t), pl.ds(pl.multiple_of(part, kt), kt)],
            send_sem=a_send.at[t, q, slot], recv_sem=a_recv.at[t, q, slot],
            device_id=(to_mp, to_x * 2 + core), device_id_type=MESH)

    def send_a(t):
        def body(q, carry):
            for order in range(3):
                a_copy(t, q, order).start()
            return carry
        lax.fori_loop(0, SLICES, body, 0)

    def sent_a(t):
        def body(q, carry):
            for order in range(3):
                a_copy(t, q, order).wait_send()
            return carry
        lax.fori_loop(0, SLICES, body, 0)

    def b_tile(src, q, n, slot):
        return pltpu.make_async_copy(
            src.at[pl.ds(pl.multiple_of(lax.rem(q, own_slices) * kt, kt), kt),
                   pl.ds(pl.multiple_of(n * nt, nt), nt)],
            b_v.at[slot], b_sem.at[slot])

    def load_tile(q, n, slot):
        @pl.when(q < own_slices)
        def _():
            b_tile(b_ref, q, n, slot).start()

        @pl.when(q >= own_slices)
        def _():
            b_tile(b_par, q, n, slot).start()

    for t in range(AHEAD):
        send_a(t)
    for j in range(B_PIECES):
        b_copy(j).start()
    for slot in range(SLOTS):
        b_tile(b_ref, 0, slot, slot).start()

    sources = [(0, half, 0), (1, half, 0), (2, half, 0), (0, half, half), (1, half, half), (2, half, half)]

    def a_loads(t, q):
        part = slice_start(q)
        mine = pl.multiple_of((mp * 2 + xx) * chip_k + part, kt)
        loads = [pltpu.make_async_copy(
            a_ref.at[chunk_rows(t), pl.ds(mine, kt)], a_v.at[q, pl.ds(0, chunk)], a_sem.at[6])]
        for i, (slot, size, off) in enumerate(sources):
            span = pl.ds(pl.multiple_of(t * chunk + off, half), half)
            loads.append(pltpu.make_async_copy(
                a_in.at[slot, span, pl.ds(pl.multiple_of(part, kt), kt)],
                a_v.at[q, pl.ds(chunk + i * half, half)], a_sem.at[i]))
        return loads

    def leg1_copies(t):
        buf = lax.rem(t, BUFS)
        return [pltpu.make_async_remote_copy(
            src_ref=acc.at[buf, pl.ds(start, chunk)], dst_ref=leg1.at[t, i],
            send_sem=l1_send.at[t, i], recv_sem=l1_recv.at[t, i],
            device_id=peer, device_id_type=MESH)
            for i, (start, peer) in enumerate(((chunk, x_peer), (chunk + 4 * half, y_peer)))]

    def leg2_copies(t):
        buf = lax.rem(t, BUFS)
        return [pltpu.make_async_remote_copy(
            src_ref=acc.at[buf, pl.ds(chunk + (2 + i) * half, half)],
            dst_ref=leg2.at[t, pl.ds(i * half, half)],
            send_sem=l2_send.at[t, i], recv_sem=l2_recv.at[t, i],
            device_id=peer, device_id_type=MESH)
            for i, peer in enumerate((y_peer, x_peer))]

    def c_copy(t):
        slot = lax.rem(t, 2)
        return pltpu.make_async_copy(c_v.at[slot], c_ref.at[chunk_rows(t)], c_sem.at[slot])

    def product(t):
        buf = lax.rem(t, BUFS)
        acc[buf] = jnp.zeros(acc.shape[1:], acc.dtype)

        def one_slice(q, carry):
            for order in range(3):
                a_copy(t, q, order).wait_recv()
            loads = a_loads(t, q)
            for load in loads:
                load.start()

            @pl.when((t == 0) & (q >= own_slices - 1) & (q < SLICES - 1))
            def _():
                def body(j, c):
                    b_copy(j).wait_recv()
                    return c
                per = B_PIECES // own_slices
                lax.fori_loop((q - own_slices + 1) * per, (q - own_slices + 2) * per, body, 0)

            for load in loads:
                load.wait()

            def columns(m, c):
                for slot in range(SLOTS):
                    n = m * SLOTS + slot
                    b_tile(b_ref, q, n, slot).wait()
                    acc[buf, :, pl.ds(pl.multiple_of(n * nt, nt), nt)] += jnp.dot(
                        a_v[q], b_v[slot], preferred_element_type=jnp.float32)
                    later = m + 1
                    wraps = later // (N_TILES // SLOTS)

                    @pl.when((t < steps - 1) | (q < SLICES - 1) | (wraps == 0))
                    def _():
                        load_tile(lax.rem(q + wraps, SLICES),
                                  (later - wraps * (N_TILES // SLOTS)) * SLOTS + slot, slot)
                return c

            lax.fori_loop(0, N_TILES // SLOTS, columns, 0)
            return carry

        lax.fori_loop(0, SLICES, one_slice, 0)

    def forward(t):
        copies = leg1_copies(t)
        for copy in copies:
            copy.wait_recv()
        loads = [pltpu.make_async_copy(
            leg1.at[t, i, pl.ds((1 - i) * half, half)], t1.at[pl.ds(i * half, half)], t_sem.at[i])
            for i in range(2)]
        for load in loads:
            load.start()
        for load in loads:
            load.wait()
        buf = lax.rem(t, BUFS)
        acc[buf, pl.ds(chunk + 2 * half, chunk)] += t1[...]
        for copy in leg2_copies(t):
            copy.start()

    def finish(t):
        loads = [pltpu.make_async_copy(
            leg1.at[t, i, pl.ds(i * half, half)], t2.at[pl.ds(i * half, half)], t_sem.at[2 + i])
            for i in range(2)]
        for load in loads:
            load.start()
        for copy in leg2_copies(t):
            copy.wait_recv()
        last = pltpu.make_async_copy(leg2.at[t], t3, t_sem.at[4])
        last.start()

        @pl.when(t >= 2)
        def _():
            c_copy(t).wait()

        for copy in leg1_copies(t) + leg2_copies(t):
            copy.wait_send()
        for load in loads:
            load.wait()
        last.wait()
        total = acc[lax.rem(t, BUFS), pl.ds(0, chunk)] + t2[...] + t3[...]
        c_v[lax.rem(t, 2)] = total.astype(c_v.dtype)
        c_copy(t).start()

    def step(s, carry):
        @pl.when(s < steps)
        def _():
            product(s)
            for copy in leg1_copies(s):
                copy.start()
            sent_a(s)

        @pl.when((s >= 1) & (s < steps + 1))
        def _():
            forward(s - 1)

        @pl.when(s + AHEAD < steps)
        def _():
            send_a(s + AHEAD)

        @pl.when(s >= 2)
        def _():
            finish(s - 2)
        return carry

    lax.fori_loop(0, steps + 2, step, 0)
    for t in (steps - 2, steps - 1):
        c_copy(t).wait()
    for j in range(B_PIECES):
        b_copy(j).wait_send()


def _product(a_rows, b_rows, chunk):
    rows = a_rows.shape[0]
    half_k, cols = b_rows.shape
    steps = rows // chunk
    nt, kt = cols // N_TILES, 2 * half_k // SLICES
    sem = pltpu.SemaphoreType.DMA
    hbm = pl.BlockSpec(memory_space=pl.ANY)
    outs = pl.pallas_call(
        functools.partial(_kernel, chunk),
        out_shape=(
            jax.ShapeDtypeStruct((rows, cols), jnp.bfloat16),
            jax.ShapeDtypeStruct((half_k, cols), jnp.bfloat16),
            jax.ShapeDtypeStruct((3, rows, 2 * half_k), jnp.bfloat16),
            jax.ShapeDtypeStruct((steps, 2, chunk, cols), jnp.float32),
            jax.ShapeDtypeStruct((steps, chunk, cols), jnp.float32),
        ),
        in_specs=[hbm] * 2,
        out_specs=(hbm,) * 5,
        scratch_shapes=[
            pltpu.VMEM((SLICES, 4 * chunk, kt), jnp.bfloat16),
            pltpu.VMEM((SLOTS, kt, nt), jnp.bfloat16),
            pltpu.VMEM((BUFS, 4 * chunk, cols), jnp.float32),
            pltpu.VMEM((chunk, cols), jnp.float32),
            pltpu.VMEM((chunk, cols), jnp.float32),
            pltpu.VMEM((chunk, cols), jnp.float32),
            pltpu.VMEM((2, chunk, cols), jnp.bfloat16),
            sem((B_PIECES,)), sem((B_PIECES,)),
            sem((steps, SLICES, 3)), sem((steps, SLICES, 3)),
            sem((steps, 2)), sem((steps, 2)), sem((steps, 2)), sem((steps, 2)),
            sem((7,)), sem((SLOTS,)), sem((5,)), sem((2,)),
        ],
        compiler_params=pltpu.CompilerParams(
            collective_id=0, has_side_effects=True, vmem_limit_bytes=60 << 20),
    )(a_rows, b_rows)
    return outs[0]


def solution(mesh):
    spec = P(("mp", "dp"), None)

    def local(a_rows, b_rows):
        return _product(a_rows, b_rows, min(64, a_rows.shape[0] // 4))

    return jax.shard_map(local, mesh=mesh, in_specs=(spec, spec), out_specs=spec, check_vma=False)
```

time: 2070 us -> 1010 us (0.49)
  Pallas kernels: 0 us -> 999 us
  waiting for transfers between devices: 784 us -> 0 us
  blocking collectives: 755 us -> 0 us
  matrix products: 298 us -> 0 us
  local copies, waits for them, and re-layouts: 210 us -> 4.7 us
    pallas_call x0 -> x1, Pallas kernels: none -> 999 us  [_product(): pl.pallas_call(functools.partial(_kernel, chunk), out_shape=(jax.ShapeDty...]
    all_to_all x1 -> x0, blocking collectives: 755 us -> none  [local_product(): a_cols = lax.all_to_all(a_split, 'dp', 2, 0, tiled=True)]
    all_gather x1 -> x0, waiting for transfers between devices: 557 us -> none  [local_product(): b_group = lax.all_gather(b_rows, 'mp', axis=0, tiled=False)]
    dot_general x1 -> x0, matrix products: 298 us -> none  [local_product(): jnp.einsum('rit,itn->rn', a_cols, b_group, preferred_element_type=jnp.flo...]
    reduce_scatter x1 -> x0, waiting for transfers between devices: 226 us -> none  [local_product(): row_sum = lax.psum_scatter(part_sum, 'dp', scatter_dimension=0, tiled=True)]
    unnamed x1, local copies, waits for them, and re-layouts: 86.6 us -> 4.7 us
    reshape x1 -> x0, local copies, waits for them, and re-layouts: 79.1 us -> none  [local_product(): a_split = a_rows.reshape(row_count, mp_size, dp_size, tok_piece)]
    all_to_all x1 -> x0, local copies, waits for them, and re-layouts: 44.6 us -> none  [local_product(): a_cols = lax.all_to_all(a_split, 'dp', 2, 0, tiled=True)]
  transfers between devices with their start and end apart: 2 -> 0, of which waited for: 2 -> 0; matrix products, arithmetic and copies ran while one was open for 10% -> 0% of each run, Pallas kernels for 0% -> 0%
where the time goes in v2:
time: 1010 us; the launch traced here: 1000 us
  Pallas kernels  999 us (99%)
    pallas_call x1, Pallas kernels, _product(): pl.pallas_call(functools.partial(_kernel, chunk), out_shape=(jax.ShapeDty...  999 us

profile of v2, /device:TPU:0, one launch (start us, length us, event | category | flops | bytes accessed | tf_op | source)
XLA Modules:
  0.0 1003.6 jit_solution(2262750350678459176)
XLA Ops:
  0.0 998.9 %shard_map.28 = (bf16[512,4096]{1,0:T(8,128)(2,1)}, bf16[8192,4096]{1,0:T(8,128)(2,1)}, bf16[3,512,16384]{2,1,0:T(8,128)(2,1)}, f32[8,2,64,4096]{3,2,1,0:T(8,128)}, f32[8,64,4096]{2,1,0:T(8,128)}) custom-call(bf16[512,65536]{1,0:T(8,128)(2,1)} %a_ref.1, bf16[8192,4096]{1,0:T(8,128)(2,1)} %b_ref.1), custom_call_target="tpu_custom_call" | custom-call | tf_op jit(solution)/shard_map/pallas_call | solution.py:265
  998.9 4.7 copy.4

commit v3 on v2

--- a/solution.py
+++ b/solution.py
@@ -16,10 +16,10 @@
 B_PIECES = 8
 
 
-def _kernel(chunk, a_ref, b_ref, c_ref, b_par, a_in, leg1, leg2,
-            a_v, b_v, acc, t1, t2, t3, c_v,
+def _kernel(chunk, a_ref, b_ref, c_ref, b_par, a_in, leg1,
+            a_v, b_v, acc, t1, t2, leg2,
             bx_send, bx_recv, a_send, a_recv, l1_send, l1_recv, l2_send, l2_recv,
-            a_sem, b_sem, t_sem, c_sem):
+            a_sem, b_sem, t_sem):
     rows = a_ref.shape[0]
     half_k, cols = b_ref.shape
     chip_k = 2 * half_k
@@ -141,10 +141,6 @@
             device_id=peer, device_id_type=MESH)
             for i, peer in enumerate((y_peer, x_peer))]
 
-    def c_copy(t):
-        slot = lax.rem(t, 2)
-        return pltpu.make_async_copy(c_v.at[slot], c_ref.at[chunk_rows(t)], c_sem.at[slot])
-
     def product(t):
         buf = lax.rem(t, BUFS)
         acc[buf] = jnp.zeros(acc.shape[1:], acc.dtype)
@@ -209,23 +205,14 @@
             for i in range(2)]
         for load in loads:
             load.start()
+        for load in loads:
+            load.wait()
         for copy in leg2_copies(t):
             copy.wait_recv()
-        last = pltpu.make_async_copy(leg2.at[t], t3, t_sem.at[4])
-        last.start()
-
-        @pl.when(t >= 2)
-        def _():
-            c_copy(t).wait()
-
+        total = acc[lax.rem(t, BUFS), pl.ds(0, chunk)] + t2[...] + leg2[t]
+        c_ref[chunk_rows(t)] = total.astype(c_ref.dtype)
         for copy in leg1_copies(t) + leg2_copies(t):
             copy.wait_send()
-        for load in loads:
-            load.wait()
-        last.wait()
-        total = acc[lax.rem(t, BUFS), pl.ds(0, chunk)] + t2[...] + t3[...]
-        c_v[lax.rem(t, 2)] = total.astype(c_v.dtype)
-        c_copy(t).start()
 
     def step(s, carry):
         @pl.when(s < steps)
@@ -249,8 +236,6 @@
         return carry
 
     lax.fori_loop(0, steps + 2, step, 0)
-    for t in (steps - 2, steps - 1):
-        c_copy(t).wait()
     for j in range(B_PIECES):
         b_copy(j).wait_send()
 
@@ -265,29 +250,27 @@
     outs = pl.pallas_call(
         functools.partial(_kernel, chunk),
         out_shape=(
-            jax.ShapeDtypeStruct((rows, cols), jnp.bfloat16),
+            pltpu.VMEM((rows, cols), jnp.bfloat16),
             jax.ShapeDtypeStruct((half_k, cols), jnp.bfloat16),
             jax.ShapeDtypeStruct((3, rows, 2 * half_k), jnp.bfloat16),
             jax.ShapeDtypeStruct((steps, 2, chunk, cols), jnp.float32),
-            jax.ShapeDtypeStruct((steps, chunk, cols), jnp.float32),
         ),
         in_specs=[hbm] * 2,
-        out_specs=(hbm,) * 5,
+        out_specs=(pl.BlockSpec(memory_space=pltpu.VMEM),) + (hbm,) * 3,
         scratch_shapes=[
             pltpu.VMEM((SLICES, 4 * chunk, kt), jnp.bfloat16),
             pltpu.VMEM((SLOTS, kt, nt), jnp.bfloat16),
             pltpu.VMEM((BUFS, 4 * chunk, cols), jnp.float32),
             pltpu.VMEM((chunk, cols), jnp.float32),
             pltpu.VMEM((chunk, cols), jnp.float32),
-            pltpu.VMEM((chunk, cols), jnp.float32),
-            pltpu.VMEM((2, chunk, cols), jnp.bfloat16),
+            pltpu.VMEM((steps, chunk, cols), jnp.float32),
             sem((B_PIECES,)), sem((B_PIECES,)),
             sem((steps, SLICES, 3)), sem((steps, SLICES, 3)),
             sem((steps, 2)), sem((steps, 2)), sem((steps, 2)), sem((steps, 2)),
-            sem((7,)), sem((SLOTS,)), sem((5,)), sem((2,)),
+            sem((7,)), sem((SLOTS,)), sem((4,)),
         ],
         compiler_params=pltpu.CompilerParams(
-            collective_id=0, has_side_effects=True, vmem_limit_bytes=60 << 20),
+            collective_id=0, has_side_effects=True, vmem_limit_bytes=56 << 20),
     )(a_rows, b_rows)
     return outs[0]
 

time: 1010 us -> 1000 us (0.990)
  no operation moved by 1% of the time
where the time goes in v3:
time: 1000 us; the launch traced here: 999 us
  Pallas kernels  997 us (100%)
    pallas_call x1, Pallas kernels, _product(): pl.pallas_call(functools.partial(_kernel, chunk), out_shape=(pltpu.VMEM((...  997 us

profile of v3, /device:TPU:0, one launch (start us, length us, event | category | flops | bytes accessed | tf_op | source)
XLA Modules:
  0.0 998.9 jit_solution(7985260066147470325)
XLA Ops:
  0.0 996.9 %shard_map.28 = (bf16[512,4096]{1,0:T(8,128)(2,1)S(1)}, bf16[8192,4096]{1,0:T(8,128)(2,1)}, bf16[3,512,16384]{2,1,0:T(8,128)(2,1)}, f32[8,2,64,4096]{3,2,1,0:T(8,128)}) custom-call(bf16[512,65536]{1,0:T(8,128)(2,1)} %a_ref.1, bf16[8192,4096]{1,0:T(8,128)(2,1)} %b_ref.1), custom_call_target="tpu_custom_call" | custom-call | tf_op jit(solution)/shard_map/pallas_call | solution.py:250
  996.9 2.0 copy.4

commit v4 on v3

--- a/solution.py
+++ b/solution.py
@@ -19,7 +19,7 @@
 def _kernel(chunk, a_ref, b_ref, c_ref, b_par, a_in, leg1,
             a_v, b_v, acc, t1, t2, leg2,
             bx_send, bx_recv, a_send, a_recv, l1_send, l1_recv, l2_send, l2_recv,
-            a_sem, b_sem, t_sem):
+            a_sem, b_sem, t_sem, diag_sem):
     rows = a_ref.shape[0]
     half_k, cols = b_ref.shape
     chip_k = 2 * half_k
@@ -35,13 +35,12 @@
     xx = dp // 2
     x_peer = (mp, (1 - xx) * 2 + core)
     y_peer = (1 - mp, dp)
-    diagonal = (1 - mp, (1 - xx) * 2 + core)
     partner = (mp, xx * 2 + 1 - core)
 
     barrier = pltpu.get_barrier_semaphore()
-    for peer in (x_peer, y_peer, diagonal, partner):
+    for peer in (x_peer, y_peer, partner):
         pl.semaphore_signal(barrier, inc=1, device_id=peer, device_id_type=MESH)
-    pl.semaphore_wait(barrier, 4)
+    pl.semaphore_wait(barrier, 3)
 
     def chunk_rows(t):
         return pl.ds(pl.multiple_of(t * chunk, chunk), chunk)
@@ -62,6 +61,9 @@
 
     def a_copy(t, q, order):
         slot = 2 if order == 2 else (core if order == 0 else 1 - core)
+        return a_copy_to(t, q, slot)
+
+    def a_copy_to(t, q, slot):
         is_x = 1 - slot // 2
         is_y = (slot + 1) // 2
         to_mp = mp + is_y * (1 - 2 * mp)
@@ -74,12 +76,12 @@
             send_sem=a_send.at[t, q, slot], recv_sem=a_recv.at[t, q, slot],
             device_id=(to_mp, to_x * 2 + core), device_id_type=MESH)
 
-    def send_a(t):
+    def send_a(t, first=0):
         def body(q, carry):
             for order in range(3):
                 a_copy(t, q, order).start()
             return carry
-        lax.fori_loop(0, SLICES, body, 0)
+        lax.fori_loop(first, SLICES, body, 0)
 
     def sent_a(t):
         def body(q, carry):
@@ -103,7 +105,13 @@
         def _():
             b_tile(b_par, q, n, slot).start()
 
-    for t in range(AHEAD):
+    a_copy_to(0, 0, 0).start()
+    a_copy_to(0, 0, 2).start()
+    pl.semaphore_signal(diag_sem, inc=1, device_id=y_peer, device_id_type=MESH)
+    pl.semaphore_wait(diag_sem, 1)
+    a_copy_to(0, 0, 1).start()
+    send_a(0, 1)
+    for t in range(1, AHEAD):
         send_a(t)
     for j in range(B_PIECES):
         b_copy(j).start()
@@ -267,7 +275,7 @@
             sem((B_PIECES,)), sem((B_PIECES,)),
             sem((steps, SLICES, 3)), sem((steps, SLICES, 3)),
             sem((steps, 2)), sem((steps, 2)), sem((steps, 2)), sem((steps, 2)),
-            sem((7,)), sem((SLOTS,)), sem((4,)),
+            sem((7,)), sem((SLOTS,)), sem((4,)), pltpu.SemaphoreType.REGULAR,
         ],
         compiler_params=pltpu.CompilerParams(
             collective_id=0, has_side_effects=True, vmem_limit_bytes=56 << 20),

time: 1000 us -> 1000 us (level)
  no operation moved by 1% of the time
where the time goes in v4:
time: 1000 us; the launch traced here: 999 us
  Pallas kernels  997 us (100%)
    pallas_call x1, Pallas kernels, _product(): pl.pallas_call(functools.partial(_kernel, chunk), out_shape=(pltpu.VMEM((...  997 us

profile of v4, /device:TPU:0, one launch (start us, length us, event | category | flops | bytes accessed | tf_op | source)
XLA Modules:
  0.0 998.9 jit_solution(1859615484815134138)
XLA Ops:
  0.0 996.9 %shard_map.28 = (bf16[512,4096]{1,0:T(8,128)(2,1)S(1)}, bf16[8192,4096]{1,0:T(8,128)(2,1)}, bf16[3,512,16384]{2,1,0:T(8,128)(2,1)}, f32[8,2,64,4096]{3,2,1,0:T(8,128)}) custom-call(bf16[512,65536]{1,0:T(8,128)(2,1)} %a_ref.1, bf16[8192,4096]{1,0:T(8,128)(2,1)} %b_ref.1), custom_call_target="tpu_custom_call" | custom-call | tf_op jit(solution)/shard_map/pallas_call | solution.py:258
  996.9 2.0 copy.4

commit v5 on v3

--- a/solution.py
+++ b/solution.py
@@ -13,13 +13,14 @@
 SLOTS = 4
 AHEAD = 2
 BUFS = 3
+RING = 4
 B_PIECES = 8
 
 
-def _kernel(chunk, a_ref, b_ref, c_ref, b_par, a_in, leg1,
-            a_v, b_v, acc, t1, t2, leg2,
+def _kernel(chunk, a_ref, b_ref, c_ref, b_par, a_in,
+            a_v, b_v, acc, leg1, leg2,
             bx_send, bx_recv, a_send, a_recv, l1_send, l1_recv, l2_send, l2_recv,
-            a_sem, b_sem, t_sem):
+            a_sem, b_sem):
     rows = a_ref.shape[0]
     half_k, cols = b_ref.shape
     chip_k = 2 * half_k
@@ -116,18 +117,19 @@
         part = slice_start(q)
         mine = pl.multiple_of((mp * 2 + xx) * chip_k + part, kt)
         loads = [pltpu.make_async_copy(
-            a_ref.at[chunk_rows(t), pl.ds(mine, kt)], a_v.at[q, pl.ds(0, chunk)], a_sem.at[6])]
+            a_ref.at[chunk_rows(t), pl.ds(mine, kt)], a_v.at[q, pl.ds(0, chunk)],
+            a_sem.at[lax.rem(q, 2), 6])]
         for i, (slot, size, off) in enumerate(sources):
             span = pl.ds(pl.multiple_of(t * chunk + off, half), half)
             loads.append(pltpu.make_async_copy(
                 a_in.at[slot, span, pl.ds(pl.multiple_of(part, kt), kt)],
-                a_v.at[q, pl.ds(chunk + i * half, half)], a_sem.at[i]))
+                a_v.at[q, pl.ds(chunk + i * half, half)], a_sem.at[lax.rem(q, 2), i]))
         return loads
 
     def leg1_copies(t):
         buf = lax.rem(t, BUFS)
         return [pltpu.make_async_remote_copy(
-            src_ref=acc.at[buf, pl.ds(start, chunk)], dst_ref=leg1.at[t, i],
+            src_ref=acc.at[buf, pl.ds(start, chunk)], dst_ref=leg1.at[lax.rem(t, RING), i],
             send_sem=l1_send.at[t, i], recv_sem=l1_recv.at[t, i],
             device_id=peer, device_id_type=MESH)
             for i, (start, peer) in enumerate(((chunk, x_peer), (chunk + 4 * half, y_peer)))]
@@ -136,7 +138,7 @@
         buf = lax.rem(t, BUFS)
         return [pltpu.make_async_remote_copy(
             src_ref=acc.at[buf, pl.ds(chunk + (2 + i) * half, half)],
-            dst_ref=leg2.at[t, pl.ds(i * half, half)],
+            dst_ref=leg2.at[lax.rem(t, RING), pl.ds(i * half, half)],
             send_sem=l2_send.at[t, i], recv_sem=l2_recv.at[t, i],
             device_id=peer, device_id_type=MESH)
             for i, peer in enumerate((y_peer, x_peer))]
@@ -145,12 +147,18 @@
         buf = lax.rem(t, BUFS)
         acc[buf] = jnp.zeros(acc.shape[1:], acc.dtype)
 
-        def one_slice(q, carry):
+        def fetch(q):
             for order in range(3):
                 a_copy(t, q, order).wait_recv()
-            loads = a_loads(t, q)
-            for load in loads:
+            for load in a_loads(t, q):
                 load.start()
+
+        fetch(0)
+
+        def one_slice(q, carry):
+            @pl.when(q < SLICES - 1)
+            def _():
+                fetch(q + 1)
 
             @pl.when((t == 0) & (q >= own_slices - 1) & (q < SLICES - 1))
             def _():
@@ -160,7 +168,7 @@
                 per = B_PIECES // own_slices
                 lax.fori_loop((q - own_slices + 1) * per, (q - own_slices + 2) * per, body, 0)
 
-            for load in loads:
+            for load in a_loads(t, q):
                 load.wait()
 
             def columns(m, c):
@@ -184,33 +192,22 @@
         lax.fori_loop(0, SLICES, one_slice, 0)
 
     def forward(t):
-        copies = leg1_copies(t)
-        for copy in copies:
+        for copy in leg1_copies(t):
             copy.wait_recv()
-        loads = [pltpu.make_async_copy(
-            leg1.at[t, i, pl.ds((1 - i) * half, half)], t1.at[pl.ds(i * half, half)], t_sem.at[i])
-            for i in range(2)]
-        for load in loads:
-            load.start()
-        for load in loads:
-            load.wait()
-        buf = lax.rem(t, BUFS)
-        acc[buf, pl.ds(chunk + 2 * half, chunk)] += t1[...]
+        buf, slot = lax.rem(t, BUFS), lax.rem(t, RING)
+        for i in range(2):
+            acc[buf, pl.ds(chunk + (2 + i) * half, half)] += leg1[slot, i, pl.ds((1 - i) * half, half)]
         for copy in leg2_copies(t):
             copy.start()
 
     def finish(t):
-        loads = [pltpu.make_async_copy(
-            leg1.at[t, i, pl.ds(i * half, half)], t2.at[pl.ds(i * half, half)], t_sem.at[2 + i])
-            for i in range(2)]
-        for load in loads:
-            load.start()
-        for load in loads:
-            load.wait()
         for copy in leg2_copies(t):
             copy.wait_recv()
-        total = acc[lax.rem(t, BUFS), pl.ds(0, chunk)] + t2[...] + leg2[t]
-        c_ref[chunk_rows(t)] = total.astype(c_ref.dtype)
+        buf, slot = lax.rem(t, BUFS), lax.rem(t, RING)
+        for i in range(2):
+            part = pl.ds(i * half, half)
+            total = acc[buf, part] + leg1[slot, i, part] + leg2[slot, part]
+            c_ref[pl.ds(pl.multiple_of(t * chunk + i * half, half), half)] = total.astype(c_ref.dtype)
         for copy in leg1_copies(t) + leg2_copies(t):
             copy.wait_send()
 
@@ -226,13 +223,13 @@
         def _():
             forward(s - 1)
 
+        @pl.when(s >= 2)
+        def _():
+            finish(s - 2)
+
         @pl.when(s + AHEAD < steps)
         def _():
             send_a(s + AHEAD)
-
-        @pl.when(s >= 2)
-        def _():
-            finish(s - 2)
         return carry
 
     lax.fori_loop(0, steps + 2, step, 0)
@@ -253,21 +250,19 @@
             pltpu.VMEM((rows, cols), jnp.bfloat16),
             jax.ShapeDtypeStruct((half_k, cols), jnp.bfloat16),
             jax.ShapeDtypeStruct((3, rows, 2 * half_k), jnp.bfloat16),
-            jax.ShapeDtypeStruct((steps, 2, chunk, cols), jnp.float32),
         ),
         in_specs=[hbm] * 2,
-        out_specs=(pl.BlockSpec(memory_space=pltpu.VMEM),) + (hbm,) * 3,
+        out_specs=(pl.BlockSpec(memory_space=pltpu.VMEM),) + (hbm,) * 2,
         scratch_shapes=[
             pltpu.VMEM((SLICES, 4 * chunk, kt), jnp.bfloat16),
             pltpu.VMEM((SLOTS, kt, nt), jnp.bfloat16),
             pltpu.VMEM((BUFS, 4 * chunk, cols), jnp.float32),
-            pltpu.VMEM((chunk, cols), jnp.float32),
-            pltpu.VMEM((chunk, cols), jnp.float32),
-            pltpu.VMEM((steps, chunk, cols), jnp.float32),
+            pltpu.VMEM((RING, 2, chunk, cols), jnp.float32),
+            pltpu.VMEM((RING, chunk, cols), jnp.float32),
             sem((B_PIECES,)), sem((B_PIECES,)),
             sem((steps, SLICES, 3)), sem((steps, SLICES, 3)),
             sem((steps, 2)), sem((steps, 2)), sem((steps, 2)), sem((steps, 2)),
-            sem((7,)), sem((SLOTS,)), sem((4,)),
+            sem((2, 7)), sem((SLOTS,)),
         ],
         compiler_params=pltpu.CompilerParams(
             collective_id=0, has_side_effects=True, vmem_limit_bytes=56 << 20),

time: 1000 us -> 999 us (level)
  no operation moved by 1% of the time
where the time goes in v5:
time: 999 us
  Pallas kernels  997 us (100%)
    pallas_call x1, Pallas kernels, _product(): pl.pallas_call(functools.partial(_kernel, chunk), out_shape=(pltpu.VMEM((...  997 us

profile of v5, /device:TPU:0, one launch (start us, length us, event | category | flops | bytes accessed | tf_op | source)
XLA Modules:
  0.0 998.9 jit_solution(9311084190640914070)
XLA Ops:
  0.0 996.9 %shard_map.28 = (bf16[512,4096]{1,0:T(8,128)(2,1)S(1)}, bf16[8192,4096]{1,0:T(8,128)(2,1)}, bf16[3,512,16384]{2,1,0:T(8,128)(2,1)}) custom-call(bf16[512,65536]{1,0:T(8,128)(2,1)} %a_ref.1, bf16[8192,4096]{1,0:T(8,128)(2,1)} %b_ref.1), custom_call_target="tpu_custom_call" | custom-call | tf_op jit(solution)/shard_map/pallas_call | solution.py:247
  996.9 2.0 copy.4

commit v6 on v5

--- a/solution.py
+++ b/solution.py
@@ -18,9 +18,9 @@
 
 
 def _kernel(chunk, a_ref, b_ref, c_ref, b_par, a_in,
-            a_v, b_v, acc, leg1, leg2,
+            a_v, b_v, acc, leg1, leg2, stage,
             bx_send, bx_recv, a_send, a_recv, l1_send, l1_recv, l2_send, l2_recv,
-            a_sem, b_sem):
+            a_sem, b_sem, stage_sem, diag_sem):
     rows = a_ref.shape[0]
     half_k, cols = b_ref.shape
     chip_k = 2 * half_k
@@ -36,13 +36,7 @@
     xx = dp // 2
     x_peer = (mp, (1 - xx) * 2 + core)
     y_peer = (1 - mp, dp)
-    diagonal = (1 - mp, (1 - xx) * 2 + core)
     partner = (mp, xx * 2 + 1 - core)
-
-    barrier = pltpu.get_barrier_semaphore()
-    for peer in (x_peer, y_peer, diagonal, partner):
-        pl.semaphore_signal(barrier, inc=1, device_id=peer, device_id_type=MESH)
-    pl.semaphore_wait(barrier, 4)
 
     def chunk_rows(t):
         return pl.ds(pl.multiple_of(t * chunk, chunk), chunk)
@@ -61,26 +55,32 @@
             send_sem=bx_send.at[j], recv_sem=bx_recv.at[j],
             device_id=partner, device_id_type=MESH)
 
-    def a_copy(t, q, order):
-        slot = 2 if order == 2 else (core if order == 0 else 1 - core)
+    def a_place(q, slot):
         is_x = 1 - slot // 2
         is_y = (slot + 1) // 2
         to_mp = mp + is_y * (1 - 2 * mp)
         to_x = xx + is_x * (1 - 2 * xx)
-        part = slice_start(q)
+        part = pl.multiple_of(slice_start(q), kt)
         start = pl.multiple_of((to_mp * 2 + to_x) * chip_k + part, kt)
+        return part, start, (to_mp, to_x * 2 + core)
+
+    def a_copy_to(t, q, slot, src=None):
+        part, start, peer = a_place(q, slot)
         return pltpu.make_async_remote_copy(
-            src_ref=a_ref.at[chunk_rows(t), pl.ds(start, kt)],
-            dst_ref=a_in.at[slot, chunk_rows(t), pl.ds(pl.multiple_of(part, kt), kt)],
+            src_ref=a_ref.at[chunk_rows(t), pl.ds(start, kt)] if src is None else src,
+            dst_ref=a_in.at[slot, chunk_rows(t), pl.ds(part, kt)],
             send_sem=a_send.at[t, q, slot], recv_sem=a_recv.at[t, q, slot],
-            device_id=(to_mp, to_x * 2 + core), device_id_type=MESH)
-
-    def send_a(t):
+            device_id=peer, device_id_type=MESH)
+
+    def a_copy(t, q, order):
+        return a_copy_to(t, q, 2 if order == 2 else (core if order == 0 else 1 - core))
+
+    def send_a(t, first=0):
         def body(q, carry):
             for order in range(3):
                 a_copy(t, q, order).start()
             return carry
-        lax.fori_loop(0, SLICES, body, 0)
+        lax.fori_loop(first, SLICES, body, 0)
 
     def sent_a(t):
         def body(q, carry):
@@ -104,7 +104,37 @@
         def _():
             b_tile(b_par, q, n, slot).start()
 
-    for t in range(AHEAD):
+    def staged(slot):
+        start = a_place(0, slot)[1]
+        return pltpu.make_async_copy(
+            a_ref.at[chunk_rows(0), pl.ds(start, kt)], stage.at[slot], stage_sem.at[slot])
+
+    def send_first(slot):
+        @pl.when(core == 0)
+        def _():
+            staged(slot).wait()
+            a_copy_to(0, 0, slot, stage.at[slot]).start()
+
+        @pl.when(core == 1)
+        def _():
+            a_copy_to(0, 0, slot).start()
+
+    @pl.when(core == 0)
+    def _():
+        for slot in (0, 2, 1):
+            staged(slot).start()
+
+    barrier = pltpu.get_barrier_semaphore()
+    for peer in (x_peer, y_peer, partner):
+        pl.semaphore_signal(barrier, inc=1, device_id=peer, device_id_type=MESH)
+    pl.semaphore_wait(barrier, 3)
+    pl.semaphore_signal(diag_sem, inc=1, device_id=y_peer, device_id_type=MESH)
+    send_first(0)
+    send_first(2)
+    pl.semaphore_wait(diag_sem, 1)
+    send_first(1)
+    send_a(0, 1)
+    for t in range(1, AHEAD):
         send_a(t)
     for j in range(B_PIECES):
         b_copy(j).start()
@@ -201,10 +231,10 @@
             copy.start()
 
     def finish(t):
-        for copy in leg2_copies(t):
-            copy.wait_recv()
+        copies = leg2_copies(t)
         buf, slot = lax.rem(t, BUFS), lax.rem(t, RING)
         for i in range(2):
+            copies[i].wait_recv()
             part = pl.ds(i * half, half)
             total = acc[buf, part] + leg1[slot, i, part] + leg2[slot, part]
             c_ref[pl.ds(pl.multiple_of(t * chunk + i * half, half), half)] = total.astype(c_ref.dtype)
@@ -259,10 +289,11 @@
             pltpu.VMEM((BUFS, 4 * chunk, cols), jnp.float32),
             pltpu.VMEM((RING, 2, chunk, cols), jnp.float32),
             pltpu.VMEM((RING, chunk, cols), jnp.float32),
+            pltpu.VMEM((3, chunk, kt), jnp.bfloat16),
             sem((B_PIECES,)), sem((B_PIECES,)),
             sem((steps, SLICES, 3)), sem((steps, SLICES, 3)),
             sem((steps, 2)), sem((steps, 2)), sem((steps, 2)), sem((steps, 2)),
-            sem((2, 7)), sem((SLOTS,)),
+            sem((2, 7)), sem((SLOTS,)), sem((3,)), pltpu.SemaphoreType.REGULAR,
         ],
         compiler_params=pltpu.CompilerParams(
             collective_id=0, has_side_effects=True, vmem_limit_bytes=56 << 20),

time: 999 us -> 999 us (level)
  no operation moved by 1% of the time
where the time goes in v6:
time: 999 us
  Pallas kernels  997 us (100%)
    pallas_call x1, Pallas kernels, _product(): pl.pallas_call(functools.partial(_kernel, chunk), out_shape=(pltpu.VMEM((...  997 us

profile of v6, /device:TPU:0, one launch (start us, length us, event | category | flops | bytes accessed | tf_op | source)
XLA Modules:
  0.0 998.9 jit_solution(9887208606400789663)
XLA Ops:
  0.0 996.9 %shard_map.28 = (bf16[512,4096]{1,0:T(8,128)(2,1)S(1)}, bf16[8192,4096]{1,0:T(8,128)(2,1)}, bf16[3,512,16384]{2,1,0:T(8,128)(2,1)}) custom-call(bf16[512,65536]{1,0:T(8,128)(2,1)} %a_ref.1, bf16[8192,4096]{1,0:T(8,128)(2,1)} %b_ref.1), custom_call_target="tpu_custom_call" | custom-call | tf_op jit(solution)/shard_map/pallas_call | solution.py:277
  996.9 2.0 copy.4

commit v7 on v6

--- a/solution.py
+++ b/solution.py
@@ -18,9 +18,9 @@
 
 
 def _kernel(chunk, a_ref, b_ref, c_ref, b_par, a_in,
-            a_v, b_v, acc, leg1, leg2, stage,
+            a_v, b_v, acc, leg1, leg2,
             bx_send, bx_recv, a_send, a_recv, l1_send, l1_recv, l2_send, l2_recv,
-            a_sem, b_sem, stage_sem, diag_sem):
+            a_sem, b_sem, x_in, y_in, diag_in, core_in):
     rows = a_ref.shape[0]
     half_k, cols = b_ref.shape
     chip_k = 2 * half_k
@@ -64,10 +64,10 @@
         start = pl.multiple_of((to_mp * 2 + to_x) * chip_k + part, kt)
         return part, start, (to_mp, to_x * 2 + core)
 
-    def a_copy_to(t, q, slot, src=None):
+    def a_copy_to(t, q, slot):
         part, start, peer = a_place(q, slot)
         return pltpu.make_async_remote_copy(
-            src_ref=a_ref.at[chunk_rows(t), pl.ds(start, kt)] if src is None else src,
+            src_ref=a_ref.at[chunk_rows(t), pl.ds(start, kt)],
             dst_ref=a_in.at[slot, chunk_rows(t), pl.ds(part, kt)],
             send_sem=a_send.at[t, q, slot], recv_sem=a_recv.at[t, q, slot],
             device_id=peer, device_id_type=MESH)
@@ -104,38 +104,62 @@
         def _():
             b_tile(b_par, q, n, slot).start()
 
-    def staged(slot):
-        start = a_place(0, slot)[1]
-        return pltpu.make_async_copy(
-            a_ref.at[chunk_rows(0), pl.ds(start, kt)], stage.at[slot], stage_sem.at[slot])
-
-    def send_first(slot):
-        @pl.when(core == 0)
-        def _():
-            staged(slot).wait()
-            a_copy_to(0, 0, slot, stage.at[slot]).start()
-
-        @pl.when(core == 1)
-        def _():
-            a_copy_to(0, 0, slot).start()
+    def signal(semaphore, peer):
+        pl.semaphore_signal(semaphore, inc=1, device_id=peer, device_id_type=MESH)
+
+    barrier = pltpu.get_barrier_semaphore()
+
+    @pl.when(xx == 0)
+    def _():
+        signal(barrier, x_peer)
+
+    @pl.when(mp == 0)
+    def _():
+        signal(barrier, y_peer)
 
     @pl.when(core == 0)
     def _():
-        for slot in (0, 2, 1):
-            staged(slot).start()
-
-    barrier = pltpu.get_barrier_semaphore()
-    for peer in (x_peer, y_peer, partner):
-        pl.semaphore_signal(barrier, inc=1, device_id=peer, device_id_type=MESH)
-    pl.semaphore_wait(barrier, 3)
-    pl.semaphore_signal(diag_sem, inc=1, device_id=y_peer, device_id_type=MESH)
-    send_first(0)
-    send_first(2)
-    pl.semaphore_wait(diag_sem, 1)
-    send_first(1)
+        signal(barrier, partner)
+
+    @pl.when(xx + mp + core > 0)
+    def _():
+        pl.semaphore_wait(barrier, xx + mp + core)
+
+    @pl.when(xx == 1)
+    def _():
+        signal(x_in, x_peer)
+        a_copy_to(0, 0, 0).start()
+
+    @pl.when(mp == 1)
+    def _():
+        signal(y_in, y_peer)
+        a_copy_to(0, 0, 2).start()
+
+    @pl.when(core == 1)
+    def _():
+        signal(core_in, partner)
+
+    @pl.when(xx == 0)
+    def _():
+        pl.semaphore_wait(x_in, 1)
+        a_copy_to(0, 0, 0).start()
+
+    @pl.when(mp == 0)
+    def _():
+        pl.semaphore_wait(y_in, 1)
+        a_copy_to(0, 0, 2).start()
+
+    signal(diag_in, y_peer)
+    pl.semaphore_wait(diag_in, 1)
+    a_copy_to(0, 0, 1).start()
     send_a(0, 1)
     for t in range(1, AHEAD):
         send_a(t)
+
+    @pl.when(core == 0)
+    def _():
+        pl.semaphore_wait(core_in, 1)
+
     for j in range(B_PIECES):
         b_copy(j).start()
     for slot in range(SLOTS):
@@ -289,11 +313,10 @@
             pltpu.VMEM((BUFS, 4 * chunk, cols), jnp.float32),
             pltpu.VMEM((RING, 2, chunk, cols), jnp.float32),
             pltpu.VMEM((RING, chunk, cols), jnp.float32),
-            pltpu.VMEM((3, chunk, kt), jnp.bfloat16),
             sem((B_PIECES,)), sem((B_PIECES,)),
             sem((steps, SLICES, 3)), sem((steps, SLICES, 3)),
             sem((steps, 2)), sem((steps, 2)), sem((steps, 2)), sem((steps, 2)),
-            sem((2, 7)), sem((SLOTS,)), sem((3,)), pltpu.SemaphoreType.REGULAR,
+            sem((2, 7)), sem((SLOTS,)), *[pltpu.SemaphoreType.REGULAR] * 4,
         ],
         compiler_params=pltpu.CompilerParams(
             collective_id=0, has_side_effects=True, vmem_limit_bytes=56 << 20),

time: 999 us -> 998 us (level)
  no operation moved by 1% of the time
where the time goes in v7:
time: 998 us
  Pallas kernels  996 us (100%)
    pallas_call x1, Pallas kernels, _product(): pl.pallas_call(functools.partial(_kernel, chunk), out_shape=(pltpu.VMEM((...  996 us

profile of v7, /device:TPU:0, one launch (start us, length us, event | category | flops | bytes accessed | tf_op | source)
XLA Modules:
  0.0 998.3 jit_solution(18413305124658269720)
XLA Ops:
  0.0 996.2 %shard_map.28 = (bf16[512,4096]{1,0:T(8,128)(2,1)S(1)}, bf16[8192,4096]{1,0:T(8,128)(2,1)}, bf16[3,512,16384]{2,1,0:T(8,128)(2,1)}) custom-call(bf16[512,65536]{1,0:T(8,128)(2,1)} %a_ref.1, bf16[8192,4096]{1,0:T(8,128)(2,1)} %b_ref.1), custom_call_target="tpu_custom_call" | custom-call | tf_op jit(solution)/shard_map/pallas_call | solution.py:301
  996.2 2.0 copy.4

commit v8 on v7

--- a/solution.py
+++ b/solution.py
@@ -84,8 +84,12 @@
 
     def sent_a(t):
         def body(q, carry):
-            for order in range(3):
-                a_copy(t, q, order).wait_send()
+            a_copy_to(t, q, 1).wait_send()
+
+            @pl.when((t > 0) | (q > 0) | (core == 0))
+            def _():
+                for slot in (0, 2):
+                    a_copy_to(t, q, slot).wait_send()
             return carry
         lax.fori_loop(0, SLICES, body, 0)
 
@@ -117,13 +121,13 @@
     def _():
         signal(barrier, y_peer)
 
-    @pl.when(core == 0)
+    @pl.when(core == 1)
     def _():
         signal(barrier, partner)
 
-    @pl.when(xx + mp + core > 0)
-    def _():
-        pl.semaphore_wait(barrier, xx + mp + core)
+    @pl.when(xx + mp + 1 - core > 0)
+    def _():
+        pl.semaphore_wait(barrier, xx + mp + 1 - core)
 
     @pl.when(xx == 1)
     def _():
@@ -135,7 +139,7 @@
         signal(y_in, y_peer)
         a_copy_to(0, 0, 2).start()
 
-    @pl.when(core == 1)
+    @pl.when(core == 0)
     def _():
         signal(core_in, partner)
 
@@ -150,13 +154,19 @@
         a_copy_to(0, 0, 2).start()
 
     signal(diag_in, y_peer)
+
+    @pl.when(core == 1)
+    def _():
+        for slot in (0, 2):
+            a_copy_to(0, 0, slot).wait_send()
+
     pl.semaphore_wait(diag_in, 1)
     a_copy_to(0, 0, 1).start()
     send_a(0, 1)
     for t in range(1, AHEAD):
         send_a(t)
 
-    @pl.when(core == 0)
+    @pl.when(core == 1)
     def _():
         pl.semaphore_wait(core_in, 1)
 

time: 998 us -> 997 us (level)
  no operation moved by 1% of the time
where the time goes in v8:
time: 997 us
  Pallas kernels  995 us (100%)
    pallas_call x1, Pallas kernels, _product(): pl.pallas_call(functools.partial(_kernel, chunk), out_shape=(pltpu.VMEM((...  995 us

profile of v8, /device:TPU:0, one launch (start us, length us, event | category | flops | bytes accessed | tf_op | source)
XLA Modules:
  0.0 997.1 jit_solution(16526334868315004139)
XLA Ops:
  0.0 995.1 %shard_map.28 = (bf16[512,4096]{1,0:T(8,128)(2,1)S(1)}, bf16[8192,4096]{1,0:T(8,128)(2,1)}, bf16[3,512,16384]{2,1,0:T(8,128)(2,1)}) custom-call(bf16[512,65536]{1,0:T(8,128)(2,1)} %a_ref.1, bf16[8192,4096]{1,0:T(8,128)(2,1)} %b_ref.1), custom_call_target="tpu_custom_call" | custom-call | tf_op jit(solution)/shard_map/pallas_call | solution.py:311
  995.1 2.0 copy.4

commit v9 on v8

--- a/solution.py
+++ b/solution.py
@@ -84,12 +84,14 @@
 
     def sent_a(t):
         def body(q, carry):
-            a_copy_to(t, q, 1).wait_send()
-
             @pl.when((t > 0) | (q > 0) | (core == 0))
             def _():
-                for slot in (0, 2):
+                for slot in (0, 1):
                     a_copy_to(t, q, slot).wait_send()
+
+            @pl.when((t > 0) | (q > 1) | (core == 0))
+            def _():
+                a_copy_to(t, q, 2).wait_send()
             return carry
         lax.fori_loop(0, SLICES, body, 0)
 
@@ -162,7 +164,21 @@
 
     pl.semaphore_wait(diag_in, 1)
     a_copy_to(0, 0, 1).start()
-    send_a(0, 1)
+
+    @pl.when(core == 1)
+    def _():
+        a_copy_to(0, 1, 2).start()
+        a_copy_to(0, 0, 1).wait_send()
+        a_copy_to(0, 1, 2).wait_send()
+
+    for order in range(2):
+        a_copy(0, 1, order).start()
+
+    @pl.when(core == 0)
+    def _():
+        a_copy_to(0, 1, 2).start()
+
+    send_a(0, 2)
     for t in range(1, AHEAD):
         send_a(t)
 

time: 997 us -> 997 us (level)
  no operation moved by 1% of the time
where the time goes in v9:
time: 997 us; the launch traced here: 991 us
  Pallas kernels  989 us (99%)
    pallas_call x1, Pallas kernels, _product(): pl.pallas_call(functools.partial(_kernel, chunk), out_shape=(pltpu.VMEM((...  989 us

profile of v9, /device:TPU:0, one launch (start us, length us, event | category | flops | bytes accessed | tf_op | source)
XLA Modules:
  0.0 990.9 jit_solution(478776756755873158)
XLA Ops:
  0.0 988.9 %shard_map.28 = (bf16[512,4096]{1,0:T(8,128)(2,1)S(1)}, bf16[8192,4096]{1,0:T(8,128)(2,1)}, bf16[3,512,16384]{2,1,0:T(8,128)(2,1)}) custom-call(bf16[512,65536]{1,0:T(8,128)(2,1)} %a_ref.1, bf16[8192,4096]{1,0:T(8,128)(2,1)} %b_ref.1), custom_call_target="tpu_custom_call" | custom-call | tf_op jit(solution)/shard_map/pallas_call | solution.py:327
  988.9 2.0 copy.4

commit v10 on v9

--- a/solution.py
+++ b/solution.py
@@ -84,10 +84,11 @@
 
     def sent_a(t):
         def body(q, carry):
+            a_copy_to(t, q, 1).wait_send()
+
             @pl.when((t > 0) | (q > 0) | (core == 0))
             def _():
-                for slot in (0, 1):
-                    a_copy_to(t, q, slot).wait_send()
+                a_copy_to(t, q, 0).wait_send()
 
             @pl.when((t > 0) | (q > 1) | (core == 0))
             def _():
@@ -168,7 +169,6 @@
     @pl.when(core == 1)
     def _():
         a_copy_to(0, 1, 2).start()
-        a_copy_to(0, 0, 1).wait_send()
         a_copy_to(0, 1, 2).wait_send()
 
     for order in range(2):

time: 997 us -> 997 us (level)
  no operation moved by 1% of the time
where the time goes in v10:
time: 997 us; the launch traced here: 991 us
  Pallas kernels  989 us (99%)
    pallas_call x1, Pallas kernels, _product(): pl.pallas_call(functools.partial(_kernel, chunk), out_shape=(pltpu.VMEM((...  989 us

profile of v10, /device:TPU:0, one launch (start us, length us, event | category | flops | bytes accessed | tf_op | source)
XLA Modules:
  0.0 990.9 jit_solution(17671686545835715735)
XLA Ops:
  0.0 988.9 %shard_map.28 = (bf16[512,4096]{1,0:T(8,128)(2,1)S(1)}, bf16[8192,4096]{1,0:T(8,128)(2,1)}, bf16[3,512,16384]{2,1,0:T(8,128)(2,1)}) custom-call(bf16[512,65536]{1,0:T(8,128)(2,1)} %a_ref.1, bf16[8192,4096]{1,0:T(8,128)(2,1)} %b_ref.1), custom_call_target="tpu_custom_call" | custom-call | tf_op jit(solution)/shard_map/pallas_call | solution.py:327
  988.9 2.0 copy.4
